TPU v7x, 32 devices: a whole 2x2x4 slice. The times are simulated.
32 devices in a mesh: groups: 2 (over x), ctx: 16 (over z, y, core).
Axes of the slice: x: 2, y: 2, z: 4, core: 2. Of those that a mesh axis runs over, the one named last changes fastest.
Arguments:
- queries: bfloat16 [8192, 1024], P(('groups', 'ctx')), parts along dimension 0, may hold values from -7 to 7
- keys: bfloat16 [8192, 128], P(('groups', 'ctx')), parts along dimension 0, may hold values from -7 to 7
- values: bfloat16 [8192, 128], P(('groups', 'ctx')), parts along dimension 0, may hold values from -6 to 6
- span_order: int32 [64], P('groups'), parts along dimension 0, may hold values from 0 to 31, as said below
Outputs:
- attended: bfloat16 [8192, 1024], P(('groups', 'ctx')), parts along dimension 0
There are 2 independent parts, one for each index of `groups`. A program takes and returns all parts, laid end to end along the dimension named above; each array names one. Nothing has to cross between parts.
Inputs may be any that keep to these rules, and one draw needn't show every extreme that they name: A permutation: rows j * 128 to (j + 1) * 128 - 1 hold span span_order[j] of the sequence; for every j, span_order[2 j] + span_order[2 j + 1] = 31.
All inputs are finite; a program needn't handle non-finite values.
Results may differ from a plain program's by a relative error of at most 0.006.
Values may be sent and summed in bfloat16 or wider, within the bound.
No kernel may reach another device: no remote copies, remote signals or barrier semaphores. Data moves between devices by JAX's collectives and lax.ppermute only.
A program may use at most 64 MiB of HBM per device.

v0:
```python
import math
import jax
import jax.numpy as jnp
from jax import lax
from jax.sharding import PartitionSpec as P


def body(queries, keys, values, span_order):
    local_rows = queries.shape[0]
    head_size = keys.shape[1]
    heads = queries.shape[1] // head_size
    span = local_rows // 2
    device = lax.axis_index("ctx")
    key_positions = (
        span_order[:, None] * span + jnp.arange(span, dtype=jnp.int32)[None, :]
    ).reshape(-1)
    query_pos = lax.dynamic_slice_in_dim(key_positions, device * local_rows, local_rows, 0)
    query_heads = queries.reshape(local_rows, heads, head_size)
    scale = 1.0 / math.sqrt(head_size)

    def update(carry, key_blk, value_blk, key_pos):
        running, total, accum = carry
        score = (
            jnp.einsum("qhd,kd->hqk", query_heads, key_blk, preferred_element_type=jnp.float32)
            * scale
        )
        kept = key_pos[None, None, :] <= query_pos[None, :, None]
        score = jnp.where(kept, score, jnp.float32(-1e30))
        fresh = jnp.maximum(running, jnp.max(score, axis=-1))
        factor = jnp.exp(running - fresh)
        weight = jnp.where(kept, jnp.exp(score - fresh[:, :, None]), jnp.float32(0.0))
        total = total * factor + jnp.sum(weight, axis=-1)
        accum = accum * factor[:, :, None] + jnp.einsum(
            "hqk,kd->hqd",
            weight.astype(jnp.bfloat16),
            value_blk,
            preferred_element_type=jnp.float32,
        )
        return (fresh, total, accum)

    initial = (
        jnp.full((heads, local_rows), -1e30, jnp.float32),
        jnp.zeros((heads, local_rows), jnp.float32),
        jnp.zeros((heads, local_rows, head_size), jnp.float32),
    )
    key_piece = lax.all_gather(keys, "ctx", axis=0, tiled=True)
    value_piece = lax.all_gather(values, "ctx", axis=0, tiled=True)
    count = key_piece.shape[0]
    block = math.gcd(count, 512)

    def step(index, state):
        first = (index * block).astype(jnp.int32)
        key_blk = lax.dynamic_slice_in_dim(key_piece, first, block, 0)
        value_blk = lax.dynamic_slice_in_dim(value_piece, first, block, 0)
        key_pos = lax.dynamic_slice_in_dim(key_positions, first, block, 0)
        return update(state, key_blk, value_blk, key_pos)

    running, total, accum = lax.fori_loop(0, count // block, step, initial)
    mixed = accum / total[:, :, None]
    return (
        jnp.transpose(mixed, (1, 0, 2)).reshape(local_rows, heads * head_size).astype(jnp.bfloat16)
    )


def solution(mesh):
    in_specs = (
        P(("groups", "ctx"), None),
        P(("groups", "ctx"), None),
        P(("groups", "ctx"), None),
        P("groups"),
    )
    out_specs = P(("groups", "ctx"), None)
    return jax.shard_map(body, mesh=mesh, in_specs=in_specs, out_specs=out_specs, check_vma=False)
```

profile of v0, /device:TPU:0, one launch (start us, length us, event | category | flops | bytes accessed | tf_op | source)
XLA Modules:
  0.0 141.6 jit_solution(1959519106321978832)
XLA Ops:
  6.5 0.7 all-gather.3.cloned.1.call-update
  7.3 0.7 all-gather.5.cloned.1.call-update
  8.0 1.2 copy.8
  9.6 0.7 broadcast_multiply_fusion
  10.4 39.7 %all-gather.3.cloned.1.call-done = bf16[4096,128]{1,0:T(8,128)(2,1)} async-done(((bf16[256,128]{1,0:T(8,128)(2,1)}), bf16[4096,128]{1,0:T(8,128)(2,1)}) %all-gather.3.cloned.1.call-update) | async-done | bytes 1048592 | tf_op jit(solution)/shard_map/all_gather | solution.py:46
  50.1 39.0 %all-gather.5.cloned.1.call-done = bf16[4096,128]{1,0:T(8,128)(2,1)} async-done(((bf16[256,128]{1,0:T(8,128)(2,1)}), bf16[4096,128]{1,0:T(8,128)(2,1)}) %all-gather.5.cloned.1.call-update) | async-done | bytes 1048592 | tf_op jit(solution)/shard_map/all_gather | solution.py:47
  89.1 44.5 %while.18 = (s32[]{:T(128)}, f32[8,256]{1,0:T(8,128)S(1)}, f32[8,256]{1,0:T(8,128)S(1)}, f32[8,256,128]{2,1,0:T(8,128)S(1)}, s32[4096]{0:T(1024)S(1)}, /*index=5...) while((s32[]{:T(128)}, f32[8,256]{1,0:T(8,128)S(1)}, ...), condition=%wide.region_3.4_spmd.clone, body=%wide.region_0.3_spmd.clone.sunk | while | flops 551430144 | bytes 16129227 | solution.py:58
  89.4 1.7 %fusion.33 = (f32[8,256]{1,0:T(8,128)S(1)}, f32[512,256,8]{1,0,2:T(8,128)S(1)}) fusion(pred[256,512]{0,1:T(8,128)(4,1)S(1)} %broadcast_compare_fusion.2, bf16[256,8,128]{2,0,1:T(8,128)(2,1)S(1)} %get-tuple-element.319, bf16[4096,128]{1,0:T(8,128)(2,1)} %get-tuple-element.318, s32[]{:T(128)S(6)} %select_n.62), kind=kOutput, calls=%fused_computation.2.clone.1 | convolution fusion | flops 271579136 | bytes 4988932 | tf_op jit(solution)/shard_map/while/body/eval_jaxpr/qhd,kd->hqk/dot_general | solution.py:24
  91.1 1.0 fusion.34
  92.1 2.6 %fusion.36 = f32[8,256,128]{2,1,0:T(8,128)S(1)} fusion(f32[512,256,8]{1,0,2:T(8,128)S(1)} %get-tuple-element.283, f32[8,256]{1,0:T(8,128)S(1)} %select_maximum_fusion.2, pred[256,512]{0,1:T(8,128)(4,1)S(1)} %broadcast_compare_fusion.2, f32[8,256,128]{2,1,0:T(8,128)S(1)} %get-tuple-element.302, f32[8,256]{1,0:T(8,128)S(1)} %get-tuple-element.285, ...), kind=kOutput, calls=%fused_computation.7.clone.1 | convolution fusion | flops 274464768 | bytes 6569989 | tf_op jit(solution)/shard_map/while/body/eval_jaxpr/hqk,kd->hqd/dot_general | solution.py:33
  94.9 1.7 %fusion.33 = (f32[8,256]{1,0:T(8,128)S(1)}, f32[512,256,8]{1,0,2:T(8,128)S(1)}) fusion(pred[256,512]{0,1:T(8,128)(4,1)S(1)} %broadcast_compare_fusion.2, bf16[256,8,128]{2,0,1:T(8,128)(2,1)S(1)} %get-tuple-element.319, bf16[4096,128]{1,0:T(8,128)(2,1)} %get-tuple-element.318, s32[]{:T(128)S(6)} %select_n.62), kind=kOutput, calls=%fused_computation.2.clone.1 | convolution fusion | flops 271579136 | bytes 4988932 | tf_op jit(solution)/shard_map/while/body/eval_jaxpr/qhd,kd->hqk/dot_general | solution.py:24
  96.6 1.0 fusion.34
  97.7 2.6 %fusion.36 = f32[8,256,128]{2,1,0:T(8,128)S(1)} fusion(f32[512,256,8]{1,0,2:T(8,128)S(1)} %get-tuple-element.283, f32[8,256]{1,0:T(8,128)S(1)} %select_maximum_fusion.2, pred[256,512]{0,1:T(8,128)(4,1)S(1)} %broadcast_compare_fusion.2, f32[8,256,128]{2,1,0:T(8,128)S(1)} %get-tuple-element.302, f32[8,256]{1,0:T(8,128)S(1)} %get-tuple-element.285, ...), kind=kOutput, calls=%fused_computation.7.clone.1 | convolution fusion | flops 274464768 | bytes 6569989 | tf_op jit(solution)/shard_map/while/body/eval_jaxpr/hqk,kd->hqd/dot_general | solution.py:33
  100.5 1.7 %fusion.33 = (f32[8,256]{1,0:T(8,128)S(1)}, f32[512,256,8]{1,0,2:T(8,128)S(1)}) fusion(pred[256,512]{0,1:T(8,128)(4,1)S(1)} %broadcast_compare_fusion.2, bf16[256,8,128]{2,0,1:T(8,128)(2,1)S(1)} %get-tuple-element.319, bf16[4096,128]{1,0:T(8,128)(2,1)} %get-tuple-element.318, s32[]{:T(128)S(6)} %select_n.62), kind=kOutput, calls=%fused_computation.2.clone.1 | convolution fusion | flops 271579136 | bytes 4988932 | tf_op jit(solution)/shard_map/while/body/eval_jaxpr/qhd,kd->hqk/dot_general | solution.py:24
  102.2 1.0 fusion.34
  103.2 2.6 %fusion.36 = f32[8,256,128]{2,1,0:T(8,128)S(1)} fusion(f32[512,256,8]{1,0,2:T(8,128)S(1)} %get-tuple-element.283, f32[8,256]{1,0:T(8,128)S(1)} %select_maximum_fusion.2, pred[256,512]{0,1:T(8,128)(4,1)S(1)} %broadcast_compare_fusion.2, f32[8,256,128]{2,1,0:T(8,128)S(1)} %get-tuple-element.302, f32[8,256]{1,0:T(8,128)S(1)} %get-tuple-element.285, ...), kind=kOutput, calls=%fused_computation.7.clone.1 | convolution fusion | flops 274464768 | bytes 6569989 | tf_op jit(solution)/shard_map/while/body/eval_jaxpr/hqk,kd->hqd/dot_general | solution.py:33
  106.1 1.7 %fusion.33 = (f32[8,256]{1,0:T(8,128)S(1)}, f32[512,256,8]{1,0,2:T(8,128)S(1)}) fusion(pred[256,512]{0,1:T(8,128)(4,1)S(1)} %broadcast_compare_fusion.2, bf16[256,8,128]{2,0,1:T(8,128)(2,1)S(1)} %get-tuple-element.319, bf16[4096,128]{1,0:T(8,128)(2,1)} %get-tuple-element.318, s32[]{:T(128)S(6)} %select_n.62), kind=kOutput, calls=%fused_computation.2.clone.1 | convolution fusion | flops 271579136 | bytes 4988932 | tf_op jit(solution)/shard_map/while/body/eval_jaxpr/qhd,kd->hqk/dot_general | solution.py:24
  107.8 1.0 fusion.34
  108.8 2.6 %fusion.36 = f32[8,256,128]{2,1,0:T(8,128)S(1)} fusion(f32[512,256,8]{1,0,2:T(8,128)S(1)} %get-tuple-element.283, f32[8,256]{1,0:T(8,128)S(1)} %select_maximum_fusion.2, pred[256,512]{0,1:T(8,128)(4,1)S(1)} %broadcast_compare_fusion.2, f32[8,256,128]{2,1,0:T(8,128)S(1)} %get-tuple-element.302, f32[8,256]{1,0:T(8,128)S(1)} %get-tuple-element.285, ...), kind=kOutput, calls=%fused_computation.7.clone.1 | convolution fusion | flops 274464768 | bytes 6569989 | tf_op jit(solution)/shard_map/while/body/eval_jaxpr/hqk,kd->hqd/dot_general | solution.py:33
  111.6 1.7 %fusion.33 = (f32[8,256]{1,0:T(8,128)S(1)}, f32[512,256,8]{1,0,2:T(8,128)S(1)}) fusion(pred[256,512]{0,1:T(8,128)(4,1)S(1)} %broadcast_compare_fusion.2, bf16[256,8,128]{2,0,1:T(8,128)(2,1)S(1)} %get-tuple-element.319, bf16[4096,128]{1,0:T(8,128)(2,1)} %get-tuple-element.318, s32[]{:T(128)S(6)} %select_n.62), kind=kOutput, calls=%fused_computation.2.clone.1 | convolution fusion | flops 271579136 | bytes 4988932 | tf_op jit(solution)/shard_map/while/body/eval_jaxpr/qhd,kd->hqk/dot_general | solution.py:24
  113.3 1.0 fusion.34
  114.4 2.6 %fusion.36 = f32[8,256,128]{2,1,0:T(8,128)S(1)} fusion(f32[512,256,8]{1,0,2:T(8,128)S(1)} %get-tuple-element.283, f32[8,256]{1,0:T(8,128)S(1)} %select_maximum_fusion.2, pred[256,512]{0,1:T(8,128)(4,1)S(1)} %broadcast_compare_fusion.2, f32[8,256,128]{2,1,0:T(8,128)S(1)} %get-tuple-element.302, f32[8,256]{1,0:T(8,128)S(1)} %get-tuple-element.285, ...), kind=kOutput, calls=%fused_computation.7.clone.1 | convolution fusion | flops 274464768 | bytes 6569989 | tf_op jit(solution)/shard_map/while/body/eval_jaxpr/hqk,kd->hqd/dot_general | solution.py:33
  117.2 1.7 %fusion.33 = (f32[8,256]{1,0:T(8,128)S(1)}, f32[512,256,8]{1,0,2:T(8,128)S(1)}) fusion(pred[256,512]{0,1:T(8,128)(4,1)S(1)} %broadcast_compare_fusion.2, bf16[256,8,128]{2,0,1:T(8,128)(2,1)S(1)} %get-tuple-element.319, bf16[4096,128]{1,0:T(8,128)(2,1)} %get-tuple-element.318, s32[]{:T(128)S(6)} %select_n.62), kind=kOutput, calls=%fused_computation.2.clone.1 | convolution fusion | flops 271579136 | bytes 4988932 | tf_op jit(solution)/shard_map/while/body/eval_jaxpr/qhd,kd->hqk/dot_general | solution.py:24
  118.9 1.0 fusion.34
  119.9 2.6 %fusion.36 = f32[8,256,128]{2,1,0:T(8,128)S(1)} fusion(f32[512,256,8]{1,0,2:T(8,128)S(1)} %get-tuple-element.283, f32[8,256]{1,0:T(8,128)S(1)} %select_maximum_fusion.2, pred[256,512]{0,1:T(8,128)(4,1)S(1)} %broadcast_compare_fusion.2, f32[8,256,128]{2,1,0:T(8,128)S(1)} %get-tuple-element.302, f32[8,256]{1,0:T(8,128)S(1)} %get-tuple-element.285, ...), kind=kOutput, calls=%fused_computation.7.clone.1 | convolution fusion | flops 274464768 | bytes 6569989 | tf_op jit(solution)/shard_map/while/body/eval_jaxpr/hqk,kd->hqd/dot_general | solution.py:33
  122.8 1.7 %fusion.33 = (f32[8,256]{1,0:T(8,128)S(1)}, f32[512,256,8]{1,0,2:T(8,128)S(1)}) fusion(pred[256,512]{0,1:T(8,128)(4,1)S(1)} %broadcast_compare_fusion.2, bf16[256,8,128]{2,0,1:T(8,128)(2,1)S(1)} %get-tuple-element.319, bf16[4096,128]{1,0:T(8,128)(2,1)} %get-tuple-element.318, s32[]{:T(128)S(6)} %select_n.62), kind=kOutput, calls=%fused_computation.2.clone.1 | convolution fusion | flops 271579136 | bytes 4988932 | tf_op jit(solution)/shard_map/while/body/eval_jaxpr/qhd,kd->hqk/dot_general | solution.py:24
  124.5 1.0 fusion.34
  125.5 2.6 %fusion.36 = f32[8,256,128]{2,1,0:T(8,128)S(1)} fusion(f32[512,256,8]{1,0,2:T(8,128)S(1)} %get-tuple-element.283, f32[8,256]{1,0:T(8,128)S(1)} %select_maximum_fusion.2, pred[256,512]{0,1:T(8,128)(4,1)S(1)} %broadcast_compare_fusion.2, f32[8,256,128]{2,1,0:T(8,128)S(1)} %get-tuple-element.302, f32[8,256]{1,0:T(8,128)S(1)} %get-tuple-element.285, ...), kind=kOutput, calls=%fused_computation.7.clone.1 | convolution fusion | flops 274464768 | bytes 6569989 | tf_op jit(solution)/shard_map/while/body/eval_jaxpr/hqk,kd->hqd/dot_general | solution.py:33
  128.3 1.7 %fusion.33 = (f32[8,256]{1,0:T(8,128)S(1)}, f32[512,256,8]{1,0,2:T(8,128)S(1)}) fusion(pred[256,512]{0,1:T(8,128)(4,1)S(1)} %broadcast_compare_fusion.2, bf16[256,8,128]{2,0,1:T(8,128)(2,1)S(1)} %get-tuple-element.319, bf16[4096,128]{1,0:T(8,128)(2,1)} %get-tuple-element.318, s32[]{:T(128)S(6)} %select_n.62), kind=kOutput, calls=%fused_computation.2.clone.1 | convolution fusion | flops 271579136 | bytes 4988932 | tf_op jit(solution)/shard_map/while/body/eval_jaxpr/qhd,kd->hqk/dot_general | solution.py:24
  130.0 1.0 fusion.34
  131.1 2.6 %fusion.36 = f32[8,256,128]{2,1,0:T(8,128)S(1)} fusion(f32[512,256,8]{1,0,2:T(8,128)S(1)} %get-tuple-element.283, f32[8,256]{1,0:T(8,128)S(1)} %select_maximum_fusion.2, pred[256,512]{0,1:T(8,128)(4,1)S(1)} %broadcast_compare_fusion.2, f32[8,256,128]{2,1,0:T(8,128)S(1)} %get-tuple-element.302, f32[8,256]{1,0:T(8,128)S(1)} %get-tuple-element.285, ...), kind=kOutput, calls=%fused_computation.7.clone.1 | convolution fusion | flops 274464768 | bytes 6569989 | tf_op jit(solution)/shard_map/while/body/eval_jaxpr/hqk,kd->hqd/dot_general | solution.py:33
  133.7 1.1 copy_bitcast_fusion
  (48 shorter events, 2.4 us)
Async XLA Ops:
  6.5 43.6 %all-gather.3.cloned.1.call-start = ((), (), s32[]{:S(2)}) async-start(), calls=%async_computation | async-start | bytes 1114112 | tf_op jit(solution)/shard_map/all_gather | solution.py:46
  7.3 81.9 %all-gather.5.cloned.1.call-start = ((), (), s32[]{:S(2)}) async-start(), calls=%async_computation.1 | async-start | bytes 1114112 | tf_op jit(solution)/shard_map/all_gather | solution.py:47
Sparse Core Ops, SparseCore 0:
  9.5 40.5 all-gather.2
  52.3 36.8 all-gather.4
where the time goes:
time: 142 us
  waiting for transfers between devices  80.2 us (56%)
  matrix products  33.9 us (24%)
  between operations  13.5 us (10%)
  other arithmetic  11.2 us (8%)
  local copies, waits for them, and re-layouts  2.23 us (2%)
    all_gather x1, waiting for transfers between devices, body(): key_piece = lax.all_gather(keys, 'ctx', axis=0, tiled=True)  39.7 us
    all_gather x1, waiting for transfers between devices, body(): value_piece = lax.all_gather(values, 'ctx', axis=0, tiled=True)  39 us
    dot_general x8, matrix products, update(): jnp.einsum('hqk,kd->hqd', weight.astype(jnp.bfloat16), value_blk, preferr...  20.4 us
    dot_general x8, matrix products, update(): jnp.einsum('qhd,kd->hqk', query_heads, key_blk, preferred_element_type=jn...  13.5 us
    reduce_sum x8, other arithmetic, update(): total = total * factor + jnp.sum(weight, axis=-1)  8.06 us
  transfers between devices with their start and end apart: 2, of which 2 were waited for; matrix products, arithmetic and copies ran while one was open for 2% of the time, Pallas kernels for 0%

commit v1 on v0

--- a/solution.py
+++ b/solution.py
@@ -43,8 +43,11 @@
         jnp.zeros((heads, local_rows), jnp.float32),
         jnp.zeros((heads, local_rows, head_size), jnp.float32),
     )
-    key_piece = lax.all_gather(keys, "ctx", axis=0, tiled=True)
-    value_piece = lax.all_gather(values, "ctx", axis=0, tiled=True)
+    key_piece, value_piece = jnp.split(
+        lax.all_gather(jnp.concatenate([keys, values], axis=1), "ctx", axis=0, tiled=True),
+        [keys.shape[1]],
+        axis=1,
+    )
     count = key_piece.shape[0]
     block = math.gcd(count, 512)
 

time: 142 us -> 102 us (0.72)
  waiting for transfers between devices: 80.2 us -> 43.2 us
  matrix products: 33.9 us -> 26.7 us
  local copies, waits for them, and re-layouts: 2.23 us -> 4.9 us
  other arithmetic: 11.2 us -> 12.8 us
    all_gather x2 -> x1, waiting for transfers between devices: 78.8 us -> 43.2 us  [body(): lax.all_gather(jnp.concatenate([keys, values], axis=1), 'ctx', axis=0, ti...]
    dot_general x8, matrix products: 13.5 us -> 6.24 us  [update(): jnp.einsum('qhd,kd->hqk', query_heads, key_blk, preferred_element_type=jn...]
    split x0 -> x1, local copies, waits for them, and re-layouts: none -> 2.66 us  [body(): jnp.split(lax.all_gather(jnp.concatenate([keys, values], axis=1), 'ctx',...]
    concatenate x0 -> x1, other arithmetic: none -> 1.54 us  [body(): jnp.concatenate([keys, values], axis=1)]
  transfers between devices with their start and end apart: 2 -> 1, of which waited for: 2 -> 1; matrix products, arithmetic and copies ran while one was open for 2% -> 2% of each run, Pallas kernels for 0% -> 0%
where the time goes in v1:
time: 102 us
  waiting for transfers between devices  43.2 us (42%)
  matrix products  26.7 us (26%)
  between operations  13.4 us (13%)
  other arithmetic  12.8 us (13%)
  local copies, waits for them, and re-layouts  4.9 us (5%)
    all_gather x1, waiting for transfers between devices, body(): lax.all_gather(jnp.concatenate([keys, values], axis=1), 'ctx', axis=0, ti...  43.2 us
    dot_general x8, matrix products, update(): jnp.einsum('hqk,kd->hqd', weight.astype(jnp.bfloat16), value_blk, preferr...  20.4 us
    reduce_sum x8, other arithmetic, update(): total = total * factor + jnp.sum(weight, axis=-1)  8.06 us
    dot_general x8, matrix products, update(): jnp.einsum('qhd,kd->hqk', query_heads, key_blk, preferred_element_type=jn...  6.24 us
    split x1, local copies, waits for them, and re-layouts, body(): jnp.split(lax.all_gather(jnp.concatenate([keys, values], axis=1), 'ctx',...  2.66 us
  transfers between devices with their start and end apart: 1, of which 1 were waited for; matrix products, arithmetic and copies ran while one was open for 2% of the time, Pallas kernels for 0%

profile of v1, /device:TPU:0, one launch (start us, length us, event | category | flops | bytes accessed | tf_op | source)
XLA Modules:
  0.0 101.6 jit_solution(2815374030676099759)
XLA Ops:
  6.5 1.5 %pad_maximum_fusion = bf16[256,256]{1,0:T(8,128)(2,1)} fusion(bf16[256,128]{1,0:T(8,128)(2,1)} %param.8, bf16[256,128]{1,0:T(8,128)(2,1)} %param.7), kind=kLoop, calls=%fused_computation.27 | loop fusion | flops 262144 | bytes 262144 | tf_op jit(solution)/shard_map/concatenate | solution.py:47
  8.1 1.2 %copy.8 = bf16[256,1024]{0,1:T(8,128)(2,1)S(1)} copy(bf16[256,1024]{1,0:T(8,128)(2,1)} %param.6) | data formatting | bytes 1048576 | tf_op args[0]
  9.4 0.3 copy.9
  9.7 0.7 broadcast_multiply_fusion
  10.5 43.2 %all-gather.2.cloned.1.call-done = bf16[4096,256]{1,0:T(8,128)(2,1)} async-done(((bf16[256,256]{1,0:T(8,128)(2,1)}), bf16[4096,256]{1,0:T(8,128)(2,1)}) %all-gather.2.cloned.1.call-update) | async-done | bytes 2097168 | tf_op jit(solution)/shard_map/all_gather | solution.py:47
  53.7 2.7 %fusion.21 = (bf16[4096,128]{1,0:T(8,128)(2,1)}, bf16[4096,128]{1,0:T(8,128)(2,1)S(1)}) fusion(bf16[4096,256]{1,0:T(8,128)(2,1)} %all-gather.2.cloned.1.call-done), kind=kLoop, calls=%fused_computation.30 | loop fusion | bytes 4194304 | tf_op jit(solution)/shard_map/split | solution.py:46
  56.4 37.2 %while.18 = (s32[]{:T(128)}, f32[8,256]{1,0:T(8,128)S(1)}, f32[8,256]{1,0:T(8,128)S(1)}, f32[8,256,128]{2,1,0:T(8,128)S(1)}, s32[4096]{0:T(1024)S(1)}, /*index=5...) while((s32[]{:T(128)}, f32[8,256]{1,0:T(8,128)S(1)}, ...), condition=%wide.region_3.4_spmd.clone, body=%wide.region_0.3_spmd.clone.sunk | while | flops 551430144 | bytes 16129227 | solution.py:61
  56.6 0.8 fusion.34
  57.4 1.0 fusion.35
  58.4 2.6 %fusion.37 = f32[8,256,128]{2,1,0:T(8,128)S(1)} fusion(f32[512,256,8]{1,0,2:T(8,128)S(1)} %get-tuple-element.285, f32[8,256]{1,0:T(8,128)S(1)} %select_maximum_fusion.2, pred[256,512]{0,1:T(8,128)(4,1)S(1)} %broadcast_compare_fusion.2, f32[8,256,128]{2,1,0:T(8,128)S(1)} %get-tuple-element.304, f32[8,256]{1,0:T(8,128)S(1)} %get-tuple-element.287, ...), kind=kOutput, calls=%fused_computation.7.clone.1 | convolution fusion | flops 274464768 | bytes 6569989 | tf_op jit(solution)/shard_map/while/body/eval_jaxpr/hqk,kd->hqd/dot_general | solution.py:33
  61.3 0.8 fusion.34
  62.1 1.0 fusion.35
  63.1 2.6 %fusion.37 = f32[8,256,128]{2,1,0:T(8,128)S(1)} fusion(f32[512,256,8]{1,0,2:T(8,128)S(1)} %get-tuple-element.285, f32[8,256]{1,0:T(8,128)S(1)} %select_maximum_fusion.2, pred[256,512]{0,1:T(8,128)(4,1)S(1)} %broadcast_compare_fusion.2, f32[8,256,128]{2,1,0:T(8,128)S(1)} %get-tuple-element.304, f32[8,256]{1,0:T(8,128)S(1)} %get-tuple-element.287, ...), kind=kOutput, calls=%fused_computation.7.clone.1 | convolution fusion | flops 274464768 | bytes 6569989 | tf_op jit(solution)/shard_map/while/body/eval_jaxpr/hqk,kd->hqd/dot_general | solution.py:33
  65.9 0.8 fusion.34
  66.7 1.0 fusion.35
  67.7 2.6 %fusion.37 = f32[8,256,128]{2,1,0:T(8,128)S(1)} fusion(f32[512,256,8]{1,0,2:T(8,128)S(1)} %get-tuple-element.285, f32[8,256]{1,0:T(8,128)S(1)} %select_maximum_fusion.2, pred[256,512]{0,1:T(8,128)(4,1)S(1)} %broadcast_compare_fusion.2, f32[8,256,128]{2,1,0:T(8,128)S(1)} %get-tuple-element.304, f32[8,256]{1,0:T(8,128)S(1)} %get-tuple-element.287, ...), kind=kOutput, calls=%fused_computation.7.clone.1 | convolution fusion | flops 274464768 | bytes 6569989 | tf_op jit(solution)/shard_map/while/body/eval_jaxpr/hqk,kd->hqd/dot_general | solution.py:33
  70.6 0.8 fusion.34
  71.4 1.0 fusion.35
  72.4 2.6 %fusion.37 = f32[8,256,128]{2,1,0:T(8,128)S(1)} fusion(f32[512,256,8]{1,0,2:T(8,128)S(1)} %get-tuple-element.285, f32[8,256]{1,0:T(8,128)S(1)} %select_maximum_fusion.2, pred[256,512]{0,1:T(8,128)(4,1)S(1)} %broadcast_compare_fusion.2, f32[8,256,128]{2,1,0:T(8,128)S(1)} %get-tuple-element.304, f32[8,256]{1,0:T(8,128)S(1)} %get-tuple-element.287, ...), kind=kOutput, calls=%fused_computation.7.clone.1 | convolution fusion | flops 274464768 | bytes 6569989 | tf_op jit(solution)/shard_map/while/body/eval_jaxpr/hqk,kd->hqd/dot_general | solution.py:33
  75.2 0.8 fusion.34
  76.0 1.0 fusion.35
  77.1 2.6 %fusion.37 = f32[8,256,128]{2,1,0:T(8,128)S(1)} fusion(f32[512,256,8]{1,0,2:T(8,128)S(1)} %get-tuple-element.285, f32[8,256]{1,0:T(8,128)S(1)} %select_maximum_fusion.2, pred[256,512]{0,1:T(8,128)(4,1)S(1)} %broadcast_compare_fusion.2, f32[8,256,128]{2,1,0:T(8,128)S(1)} %get-tuple-element.304, f32[8,256]{1,0:T(8,128)S(1)} %get-tuple-element.287, ...), kind=kOutput, calls=%fused_computation.7.clone.1 | convolution fusion | flops 274464768 | bytes 6569989 | tf_op jit(solution)/shard_map/while/body/eval_jaxpr/hqk,kd->hqd/dot_general | solution.py:33
  79.9 0.8 fusion.34
  80.7 1.0 fusion.35
  81.7 2.6 %fusion.37 = f32[8,256,128]{2,1,0:T(8,128)S(1)} fusion(f32[512,256,8]{1,0,2:T(8,128)S(1)} %get-tuple-element.285, f32[8,256]{1,0:T(8,128)S(1)} %select_maximum_fusion.2, pred[256,512]{0,1:T(8,128)(4,1)S(1)} %broadcast_compare_fusion.2, f32[8,256,128]{2,1,0:T(8,128)S(1)} %get-tuple-element.304, f32[8,256]{1,0:T(8,128)S(1)} %get-tuple-element.287, ...), kind=kOutput, calls=%fused_computation.7.clone.1 | convolution fusion | flops 274464768 | bytes 6569989 | tf_op jit(solution)/shard_map/while/body/eval_jaxpr/hqk,kd->hqd/dot_general | solution.py:33
  84.5 0.8 fusion.34
  85.3 1.0 fusion.35
  86.4 2.6 %fusion.37 = f32[8,256,128]{2,1,0:T(8,128)S(1)} fusion(f32[512,256,8]{1,0,2:T(8,128)S(1)} %get-tuple-element.285, f32[8,256]{1,0:T(8,128)S(1)} %select_maximum_fusion.2, pred[256,512]{0,1:T(8,128)(4,1)S(1)} %broadcast_compare_fusion.2, f32[8,256,128]{2,1,0:T(8,128)S(1)} %get-tuple-element.304, f32[8,256]{1,0:T(8,128)S(1)} %get-tuple-element.287, ...), kind=kOutput, calls=%fused_computation.7.clone.1 | convolution fusion | flops 274464768 | bytes 6569989 | tf_op jit(solution)/shard_map/while/body/eval_jaxpr/hqk,kd->hqd/dot_general | solution.py:33
  89.2 0.8 fusion.34
  90.0 1.0 fusion.35
  91.0 2.6 %fusion.37 = f32[8,256,128]{2,1,0:T(8,128)S(1)} fusion(f32[512,256,8]{1,0,2:T(8,128)S(1)} %get-tuple-element.285, f32[8,256]{1,0:T(8,128)S(1)} %select_maximum_fusion.2, pred[256,512]{0,1:T(8,128)(4,1)S(1)} %broadcast_compare_fusion.2, f32[8,256,128]{2,1,0:T(8,128)S(1)} %get-tuple-element.304, f32[8,256]{1,0:T(8,128)S(1)} %get-tuple-element.287, ...), kind=kOutput, calls=%fused_computation.7.clone.1 | convolution fusion | flops 274464768 | bytes 6569989 | tf_op jit(solution)/shard_map/while/body/eval_jaxpr/hqk,kd->hqd/dot_general | solution.py:33
  93.6 1.1 %copy_bitcast_fusion = bf16[256,1024]{1,0:T(8,128)(2,1)} fusion(f32[8,256,128]{2,1,0:T(8,128)S(1)} %get-tuple-element.160, f32[8,256]{1,0:T(8,128)S(1)} %get-tuple-element.161), kind=kLoop, calls=%fused_computation.25 | loop fusion | flops 524288 | bytes 1581056 | tf_op jit(solution)/shard_map/convert_element_type | solution.py:64
  (47 shorter events, 2.1 us)
Async XLA Ops:
  6.5 47.2 %all-gather.2.cloned.1.call-start = ((), (), s32[]{:S(2)}) async-start(), calls=%async_computation | async-start | bytes 2228224 | tf_op jit(solution)/shard_map/all_gather | solution.py:47
Sparse Core Ops, SparseCore 0:
  9.5 44.1 all-gather.1
